TPU v7x, 32 devices: a whole 2x2x4 slice. The times are simulated.
32 devices in a mesh: dp: 8 (over z, x), rep: 4 (over y, core).
Axes of the slice: x: 2, y: 2, z: 4, core: 2. Of those that a mesh axis runs over, the one named last changes fastest.
Arguments:
- features: bfloat16 [5120, 8192], P('dp', 'rep'), may hold values from -6 to 6
- out_grads: bfloat16 [5120, 1024], P('dp'), may hold values from -12 to 12, as said below
- cold_sums: bfloat16 [8, 8192, 1024], P('dp', 'rep'), may hold values from -96 to 96
- weight: float32 [8192, 1024], P(('rep', 'dp')), may hold values from -3 to 3
- moment: float32 [8192, 1024], P(('rep', 'dp')), may hold values from -6 to 6
- second: float32 [8192, 1024], P(('rep', 'dp')), may hold values from 0.01 to 4
- ranks: int32 [8], replicated, may hold values from 0 to 7, each once
Outputs:
- new_weight: float32 [8192, 1024], P(('rep', 'dp'))
- new_moment: float32 [8192, 1024], P(('rep', 'dp'))
- new_second: float32 [8192, 1024], P(('rep', 'dp'))
- new_cold: bfloat16 [8, 8192, 1024], P('dp', 'rep')
- column_sq: float32 [1024], replicated
Inputs may be any that keep to these rules, and one draw needn't show every extreme that they name: `ranks`: each block number appears once. `out_grads`: column scales differ from column to column.
All inputs are finite; a program needn't handle non-finite values.
Results may differ from a plain program's by a relative error of at most 0.001.
Values sent between devices are 32-bit elements; how exact they have to be, the bound alone decides.
A program may use at most 128 MiB of HBM per device.

v0:
```python
import jax
import jax.numpy as jnp
from jax import lax
from jax.sharding import PartitionSpec as P


def body(features, out_grads, cold_sums, weight, moment, second, ranks):
    blocks = ranks.shape[0]
    hot_count = blocks // 2
    width = out_grads.shape[1]
    local_rows = features.shape[1]
    grad = lax.dot_general(
        features, out_grads, (((0,), (0,)), ((), ())), preferred_element_type=jnp.float32
    )
    local = cold_sums[0].astype(jnp.float32) + grad
    hot_block = ranks < hot_count
    hot_col = jnp.repeat(hot_block, 128)
    new_cold = jnp.where(hot_col[None, :], jnp.float32(0.0), local).astype(jnp.bfloat16)[None]
    partial_sq = jnp.sum(local * local, axis=0)
    column_sq = lax.psum(partial_sq, ("dp", "rep"))
    picker = (ranks[None, :] == jnp.arange(hot_count, dtype=jnp.int32)[:, None]).astype(jnp.float32)
    packed = jnp.einsum(
        "rbk,sb->rsk",
        local.reshape(local_rows, blocks, 128),
        picker,
        precision=lax.Precision.HIGHEST,
    )
    owned = lax.psum_scatter(
        packed.reshape(local_rows, hot_count * 128), "dp", scatter_dimension=0, tiled=True
    )
    owned_rows = owned.shape[0]
    spread = jnp.einsum(
        "rsk,sb->rbk",
        owned.reshape(owned_rows, hot_count, 128),
        picker,
        precision=lax.Precision.HIGHEST,
    )
    summed = spread.reshape(owned_rows, width)
    dp_count = lax.axis_size("dp")
    total_rows = local_rows * lax.axis_size("rep")
    rms = jnp.sqrt(column_sq / jnp.float32(total_rows * dp_count * features.shape[0]))
    clip = 1.0 / jnp.maximum(jnp.float32(1.0), rms)
    grad_mean = summed * clip[None, :] / jnp.float32(dp_count)
    moved = 0.9 * moment + 0.1 * grad_mean
    squared = 0.95 * second + 0.05 * grad_mean * grad_mean
    step_size = 0.05 * (moved / (1.0 - 0.9**10)) / (jnp.sqrt(squared / (1.0 - 0.95**10)) + 1e-08)
    new_moment = jnp.where(hot_col[None, :], moved, moment)
    new_second = jnp.where(hot_col[None, :], squared, second)
    new_weight = jnp.where(hot_col[None, :], weight - step_size, weight)
    return (new_weight, new_moment, new_second, new_cold, column_sq)


def solution(mesh):
    placed = (
        P("dp", "rep"),
        P("dp", None),
        P("dp", "rep", None),
        P(("rep", "dp"), None),
        P(("rep", "dp"), None),
        P(("rep", "dp"), None),
        P(),
    )
    return jax.shard_map(
        body,
        mesh=mesh,
        in_specs=placed,
        out_specs=(
            P(("rep", "dp"), None),
            P(("rep", "dp"), None),
            P(("rep", "dp"), None),
            P("dp", "rep", None),
            P(),
        ),
        check_vma=False,
    )
```

profile of v0, /device:TPU:0, one launch (start us, length us, event | category | flops | bytes accessed | tf_op | source)
XLA Modules:
  0.0 146.8 jit_solution(3876229552257421479)
XLA Ops:
  7.2 0.0 copy-start
  7.2 0.0 reduce-scatter.2.cloned.1.call-start
  7.2 6.6 %copy.12 = bf16[1,2048,1024]{1,2,0:T(8,128)(2,1)} copy(bf16[1,2048,1024]{2,1,0:T(8,128)(2,1)} %param.9) | data formatting | bytes 8388608 | tf_op args[2]
  13.8 0.0 copy-done
  13.8 8.0 %multiply_reduce_fusion = (f32[1024]{0:T(1024)S(1)}, f32[2048,1024]{0,1:T(8,128)}) fusion(bf16[640,2048]{1,0:T(8,128)(2,1)S(1)} %copy-done, bf16[640,1024]{1,0:T(8,128)(2,1)} %param.8, bf16[1,2048,1024]{1,2,0:T(8,128)(2,1)} %copy.12), kind=kOutput, calls=%fused_computation.2 | convolution fusion | flops 2692742144 | bytes 16519168 | tf_op jit(solution)/shard_map/dot_general | solution.py:12
  21.8 0.0 copy-start.2
  21.8 9.3 %copy.13 = f32[2048,8,128]{2,1,0:T(8,128)} copy(f32[2048,8,128]{0,2,1:T(8,128)} %bitcast.37) | data formatting | bytes 16777216 | tf_op jit(solution)/shard_map/reshape | solution.py:24
  31.1 0.0 copy-done.2
  31.1 7.4 %fusion.6 = f32[4,2048,128]{2,0,1:T(4,128)S(1)} fusion(f32[2048,8,128]{2,1,0:T(8,128)} %copy.13, s32[8]{0:T(128)S(1)} %copy-done.2), kind=kOutput, calls=%fused_computation.16 | convolution fusion | flops 100663328 | bytes 12582944 | tf_op jit(solution)/shard_map/rbk,sb->rsk/dot_general | solution.py:22
  38.6 2.4 %copy.31 = f32[256,8,4,128]{3,1,2,0:T(8,128)} copy(f32[256,8,4,128]{3,2,1,0:T(4,128)S(1)} %bitcast.39) | data formatting | bytes 8388608
  41.0 0.0 reduce-scatter.2.cloned.1.call-update
  41.0 0.1 broadcast_bitcast_fusion
  41.1 5.9 %fusion = bf16[1,2048,1024]{1,2,0:T(8,128)(2,1)} fusion(f32[2048,1024]{0,1:T(8,128)} %get-tuple-element.14, pred[1024]{0:T(1024)(128)(4,1)S(1)} %broadcast_bitcast_fusion), kind=kLoop, calls=%fused_computation.3 | loop fusion | flops 2097152 | bytes 12583936 | tf_op jit(solution)/shard_map/broadcast_in_dim | solution.py:18
  47.0 6.4 %copy.14 = bf16[1,2048,1024]{2,1,0:T(8,128)(2,1)} copy(bf16[1,2048,1024]{1,2,0:T(8,128)(2,1)} %fusion) | data formatting | bytes 8388608
  53.4 43.8 %psum.7 = f32[1024]{0:T(1024)S(1)} all-reduce(f32[1024]{0:T(1024)S(1)} %get-tuple-element.13), channel_id=1, replica_groups=mesh['dp'=8,'rep'=4] {'dp','rep'}, use_global_device_ids=true, to_apply=%region_2.3 | all-reduce | flops 1024 | bytes 8192 | tf_op jit(solution)/shard_map/psum | solution.py:20
  97.2 0.0 copy-start.1
  97.2 36.1 %reduce-scatter.2.cloned.1.call-done = f32[256,512]{1,0:T(8,128)} async-done(((f32[2048,512]{1,0:T(8,128)}), f32[256,512]{1,0:T(8,128)}) %reduce-scatter.2.cloned.1.call-update) | async-done | bytes 524304 | tf_op jit(solution)/shard_map/reduce_scatter | solution.py:28
  133.3 1.2 reshape.29
  134.5 0.7 fusion.4
  135.3 4.6 %fusion.2 = (f32[256,1024]{1,0:T(8,128)}, f32[256,1024]{1,0:T(8,128)}, f32[256,1024]{1,0:T(8,128)}) fusion(f32[256,1024]{1,0:T(8,128)} %param.12, f32[32,8,8,128]{3,2,1,0:T(8,128)S(1)} %bitcast.40, f32[1024]{0:T(1024)S(1)} %maximum_divide_fusion, pred[1024]{0:T(1024)(128)(4,1)S(1)} %broadcast_bitcast_fusion, f32[256,1024]{1,0:T(8,128)} %param.10, ...), kind=kLoop, calls=%fused_computation.10 | loop fusion | flops 4456448 | bytes 7345152 | tf_op jit(solution)/shard_map/jit(_where)/select_n | solution.py:48
  139.9 0.0 copy-done.1
  (2 shorter events, 0.0 us)
Async XLA Ops:
  7.2 6.6 %copy-start = (bf16[640,2048]{1,0:T(8,128)(2,1)S(1)}, bf16[640,2048]{1,0:T(8,128)(2,1)}, u32[]{:S(2)}) copy-start(bf16[640,2048]{1,0:T(8,128)(2,1)} %param.7) | copy-start | bytes 7864324
  7.2 126.1 %reduce-scatter.2.cloned.1.call-start = ((), (), s32[]{:S(2)}) async-start(), calls=%async_computation.1 | async-start | bytes 4718592 | tf_op jit(solution)/shard_map/reduce_scatter | solution.py:28
  21.8 9.3 %copy-start.2 = (s32[8]{0:T(128)S(1)}, s32[8]{0:T(128)}, u32[]{:S(2)}) copy-start(s32[8]{0:T(128)} %param.13) | copy-start | bytes 100
  97.2 42.7 %copy-start.1 = (f32[1024]{0:T(1024)}, f32[1024]{0:T(1024)S(1)}, u32[]{:S(2)}) copy-start(f32[1024]{0:T(1024)S(1)} %psum.7) | copy-start | bytes 12292
Sparse Core Ops, SparseCore 0:
  41.1 92.1 reduce-scatter.1
where the time goes:
time: 147 us
  blocking collectives  43.8 us (30%)
  waiting for transfers between devices  36.1 us (25%)
  local copies, waits for them, and re-layouts  26 us (18%)
  matrix products  16.2 us (11%)
  between operations  14.1 us (10%)
  other arithmetic  10.5 us (7%)
    psum x1, blocking collectives, body(): column_sq = lax.psum(partial_sq, ('dp', 'rep'))  43.8 us
    reduce_scatter x1, waiting for transfers between devices, body(): lax.psum_scatter(packed.reshape(local_rows, hot_count * 128), 'dp', scatt...  36.1 us
    unnamed x9, local copies, waits for them, and re-layouts  15.4 us
    reshape x1, local copies, waits for them, and re-layouts, body(): local.reshape(local_rows, blocks, 128)  9.3 us
    dot_general x1, matrix products, body(): lax.dot_general(features, out_grads, (((0,), (0,)), ((), ())), preferred_...  8.02 us
    dot_general x1, matrix products, body(): jnp.einsum('rbk,sb->rsk', local.reshape(local_rows, blocks, 128), picker,...  7.42 us
    broadcast_in_dim x1, other arithmetic, body(): jnp.where(hot_col[None, :], jnp.float32(0.0), local).astype(jnp.bfloat16)  5.88 us
    select_n x1, other arithmetic, body(): new_second = jnp.where(hot_col[None, :], squared, second)  4.64 us
  transfers between devices with their start and end apart: 1, of which 1 were waited for; matrix products, arithmetic and copies ran while one was open for 8% of the time, Pallas kernels for 0%

commit v1 on v0

v1 whole, which is shorter than its diff:
```python
import functools
import jax
import jax.numpy as jnp
from jax import lax
from jax.experimental import pallas as pl
from jax.experimental.pallas import tpu as pltpu
from jax.sharding import PartitionSpec as P

LANES = 128
SUB = 2
VMEM_GRANT = 30 * 2**20
MESH = pl.DeviceIdType.MESH


def bits_of(size):
    return max(size.bit_length() - 1, 0)


def flipped(index, bit):
    step = 1 << bit
    return index + step - 2 * step * ((index // step) % 2)


def exchange_kernel(
    n, reps, hot,
    ranks, feat, og, cold, weight, moment, second,
    summed, sq_out, nc_out, w_out, m_out, s_out,
    feat_v, og_v, cold_v, local, pack, rx, lbuf, rbuf, hsrc, hbuf,
    in_sem, state_sem, send1, recv1, zsend, lrecv, rrecv, hsend, hrecv,
):
    m = n // 2
    rows, width = cold.shape[1], cold.shape[2]
    blocks = width // LANES
    own = rows // n
    chunk = max(own, LANES)
    chunks = rows // chunk
    part = own // SUB
    me = lax.axis_index("dp")
    rep = lax.axis_index("rep")
    x = me % 2
    p = me // 2
    partner = me + 1 - 2 * x
    dp_bits, rep_bits = bits_of(n), bits_of(reps)
    steps = [("dp", b) for b in range(dp_bits)] + [("rep", b) for b in range(rep_bits)]

    half = max(m // 2, 1)
    flip = p // half if m > 1 else 0
    pr = p + flip * (m - 1 - 2 * p)

    def dest(k):
        if m == 1:
            return 0 * k
        late = (k + pr) // (m - 1)
        near = (1 - late) * (m - 1 - k) + late * (k + pr - (m - 1))
        last = k // (m - 1)
        near = (1 - last) * near + last * pr
        return near + flip * (m - 1 - 2 * near)

    def chunk_at(i):
        if chunk != own:
            return i
        k = i % m
        side = i // m
        return 2 * dest(k) + (1 - side) * (1 - x) + side * x

    def hop(axis, b):
        index = me if axis == "dp" else rep
        return {axis: flipped(index, b)}

    barrier = pltpu.get_barrier_semaphore()
    pl.semaphore_signal(barrier, inc=1, device_id={"dp": partner}, device_id_type=MESH)

    @pl.when(p > 0)
    def _():
        pl.semaphore_signal(barrier, inc=1, device_id={"dp": me - 2}, device_id_type=MESH)

    @pl.when(p < m - 1)
    def _():
        pl.semaphore_signal(barrier, inc=1, device_id={"dp": me + 2}, device_id_type=MESH)

    for axis, b in steps[1:]:
        pl.semaphore_signal(barrier, inc=1, device_id=hop(axis, b), device_id_type=MESH)

    def feat_copy(i):
        c = chunk_at(i)
        cols = pl.ds(pl.multiple_of(c * chunk, LANES), chunk)
        return pltpu.make_async_copy(feat.at[:, cols], feat_v.at[i], in_sem.at[0, i])

    def cold_copy(i):
        c = chunk_at(i)
        at = pl.ds(pl.multiple_of(c * chunk, LANES), chunk)
        return pltpu.make_async_copy(cold.at[0, at], cold_v.at[i], in_sem.at[1, i])

    state = [
        pltpu.make_async_copy(src, dst, state_sem.at[i])
        for i, (src, dst) in enumerate(
            ((weight, w_out), (moment, m_out), (second, s_out), (og, og_v))
        )
    ]
    feat_copy(0).start()
    state[3].start()
    cold_copy(0).start()

    def fetch(i, carry):
        feat_copy(i).start()
        cold_copy(i).start()
        return carry

    lax.fori_loop(1, chunks, fetch, 0)
    for copy in state[:3]:
        copy.start()

    hsrc[0] = jnp.zeros_like(hsrc[0])
    keep = [
        jnp.minimum(jnp.maximum(ranks[b] - (hot - 1), 0), 1).astype(jnp.float32)
        for b in range(blocks)
    ]
    picks = []
    for s in range(hot):
        row = []
        for b in range(blocks):
            gap = ranks[b] - s
            row.append((1 - jnp.minimum(gap * gap, 1)).astype(jnp.float32))
        picks.append(row)

    def cross(k, sub):
        d = dest(k)
        src = pl.ds(pl.multiple_of((2 * d + 1 - x) * own + sub * part, 8), part)
        dst = pl.ds(pl.multiple_of(d * own + sub * part, 8), part)
        return pltpu.make_async_remote_copy(
            src_ref=pack.at[src], dst_ref=rx.at[dst],
            send_sem=send1.at[d, sub], recv_sem=recv1.at[d, sub],
            device_id={"dp": partner}, device_id_type=MESH,
        )

    def along(d, sub, right):
        src = pl.ds(pl.multiple_of((2 * d + x) * own + sub * part, 8), part)
        dst = pl.ds(pl.multiple_of(d * own + sub * part, 8), part)
        return pltpu.make_async_remote_copy(
            src_ref=pack.at[src], dst_ref=(lbuf if right else rbuf).at[dst],
            send_sem=zsend.at[d, sub], recv_sem=(lrecv if right else rrecv).at[d, sub],
            device_id={"dp": me + 2 if right else me - 2}, device_id_type=MESH,
        )

    def norm_copy(s):
        return pltpu.make_async_remote_copy(
            src_ref=hsrc.at[s], dst_ref=hbuf.at[s],
            send_sem=hsend.at[s], recv_sem=hrecv.at[s],
            device_id=hop(*steps[s]), device_id_type=MESH,
        )

    greeted = 1 + (len(steps) - 1) + (p + m - 1) // m + (2 * m - 2 - p) // m
    pl.semaphore_wait(barrier, greeted)
    state[3].wait()

    def compute(i, carry):
        c = chunk_at(i)
        feat_copy(i).wait()
        cold_copy(i).wait()
        local[...] = lax.dot_general(
            feat_v[i], og_v[...], (((0,), (0,)), ((), ())),
            preferred_element_type=jnp.float32,
        ) + cold_v[i].astype(jnp.float32)
        at = pl.ds(pl.multiple_of(c * chunk, LANES), chunk)
        for s in range(hot):
            picked = local[:, :LANES] * picks[s][0]
            for b in range(1, blocks):
                picked += local[:, b * LANES:(b + 1) * LANES] * picks[s][b]
            pack[at, s * LANES:(s + 1) * LANES] = picked
        if chunk == own:
            @pl.when(i < m)
            def _():
                for sub in range(SUB):
                    cross(i % m, sub).start()
        for b in range(blocks):
            cols = slice(b * LANES, (b + 1) * LANES)
            values = local[:, cols]
            hsrc[0, b:b + 1, :] += jnp.sum(values * values, axis=0, keepdims=True)
            nc_out[0, at, cols] = (values * keep[b]).astype(jnp.bfloat16)
        return carry

    lax.fori_loop(0, chunks, compute, 0)
    if chunk != own:
        def launch(k, carry):
            for sub in range(SUB):
                cross(k, sub).start()
            return carry

        lax.fori_loop(0, m, launch, 0)
    norm_copy(0).start()

    def process(k, sub):
        d = dest(k)
        mine = pl.ds(pl.multiple_of((2 * d + x) * own + sub * part, 8), part)
        slot = pl.ds(pl.multiple_of(d * own + sub * part, 8), part)
        cross(k, sub).wait_recv()
        pack[mine] += rx[slot]

        @pl.when(jnp.logical_and(d >= p, p > 0))
        def _():
            along(d, sub, True).wait_recv()
            pack[mine] += lbuf[slot]

        @pl.when(jnp.logical_and(d <= p, p < m - 1))
        def _():
            along(d, sub, False).wait_recv()
            pack[mine] += rbuf[slot]

        @pl.when(d > p)
        def _():
            along(d, sub, True).start()

        @pl.when(d < p)
        def _():
            along(d, sub, False).start()

        @pl.when(d == p)
        def _():
            summed[sub * part:(sub + 1) * part] = pack[mine]

    def norm_step(s):
        norm_copy(s).wait_recv()
        hsrc[s + 1] = hsrc[s] + hbuf[s]
        if s + 1 < len(steps):
            norm_copy(s + 1).start()

    done = 0
    if m <= 8:
        for k in range(m):
            for sub in range(SUB):
                if done < len(steps):
                    norm_step(done)
                    done += 1
                process(k, sub)
    else:
        def walk(k, carry):
            for sub in range(SUB):
                process(k, sub)
            return carry

        lax.fori_loop(0, m, walk, 0)
    for s in range(done, len(steps)):
        norm_step(s)
    sq_out[...] = hsrc[len(steps)]

    for copy in state[:3]:
        copy.wait()

    def drain(k, carry):
        d = dest(k)
        for sub in range(SUB):
            cross(k, sub).wait_send()

            @pl.when(d > p)
            def _():
                along(d, sub, True).wait_send()

            @pl.when(d < p)
            def _():
                along(d, sub, False).wait_send()
        return carry

    lax.fori_loop(0, m, drain, 0)
    for s in range(len(steps)):
        norm_copy(s).wait_send()


def update_kernel(
    n, total_rows, tokens, hot,
    ranks, summed, sq, nc, weight, moment, second,
    w_hbm, m_hbm, s_hbm, nc_hbm,
    fresh, nc_sem, sem,
):
    rows, width = weight.shape
    blocks = width // LANES
    cold_out = pltpu.make_async_copy(nc, nc_hbm, nc_sem)
    cold_out.start()
    for b in range(blocks):
        cols = slice(b * LANES, (b + 1) * LANES)
        slot = ranks[b]

        @pl.when(slot < hot)
        def _():
            total = sq[b:b + 1, :]
            rms = jnp.sqrt(total / jnp.float32(total_rows * n * tokens))
            clip = 1.0 / jnp.maximum(jnp.float32(1.0), rms)
            at = pl.ds(pl.multiple_of(slot * LANES, LANES), LANES)
            grad = summed[:, at] * clip / jnp.float32(n)
            moved = 0.9 * moment[:, cols] + 0.1 * grad
            squared = 0.95 * second[:, cols] + 0.05 * grad * grad
            fresh[1, :, cols] = moved
            fresh[2, :, cols] = squared
            step = 0.05 * (moved / (1.0 - 0.9**10)) / (
                jnp.sqrt(squared / (1.0 - 0.95**10)) + 1e-08
            )
            fresh[0, :, cols] = weight[:, cols] - step

        @pl.when(slot >= hot)
        def _():
            fresh[0, :, cols] = weight[:, cols]
            fresh[1, :, cols] = moment[:, cols]
            fresh[2, :, cols] = second[:, cols]

    copies = [
        pltpu.make_async_copy(fresh.at[i], dst, sem.at[i])
        for i, dst in enumerate((w_hbm, m_hbm, s_hbm))
    ]
    for copy in copies:
        copy.start()
    for copy in copies:
        copy.wait()
    cold_out.wait()


def body(n, reps, features, out_grads, cold_sums, weight, moment, second, ranks):
    tokens, rows = features.shape
    width = out_grads.shape[1]
    blocks = ranks.shape[0]
    hot = blocks // 2
    packed = hot * LANES
    m = n // 2
    own = rows // n
    chunk = max(own, LANES)
    chunks = rows // chunk
    hops = bits_of(n) + bits_of(reps)
    f32, bf16 = jnp.float32, jnp.bfloat16
    vmem = pl.BlockSpec(memory_space=pltpu.VMEM)
    smem = pl.BlockSpec(memory_space=pltpu.SMEM)
    hbm = pl.BlockSpec(memory_space=pl.ANY)
    dma = pltpu.SemaphoreType.DMA
    summed, sq, kept, w, mo, se = pl.pallas_call(
        functools.partial(exchange_kernel, n, reps, hot),
        out_shape=(
            pltpu.VMEM((own, packed), f32),
            pltpu.VMEM((blocks, LANES), f32),
            pltpu.VMEM(cold_sums.shape, bf16),
            pltpu.VMEM(weight.shape, f32),
            pltpu.VMEM(weight.shape, f32),
            pltpu.VMEM(weight.shape, f32),
        ),
        in_specs=[smem] + [pl.BlockSpec(memory_space=pltpu.HBM)] * 6,
        out_specs=(vmem,) * 6,
        scratch_shapes=[
            pltpu.VMEM((chunks, tokens, chunk), bf16),
            pltpu.VMEM((tokens, width), bf16),
            pltpu.VMEM((chunks, chunk, width), bf16),
            pltpu.VMEM((chunk, width), f32),
            pltpu.VMEM((rows, packed), f32),
            pltpu.VMEM((m * own, packed), f32),
            pltpu.VMEM((m * own, packed), f32),
            pltpu.VMEM((m * own, packed), f32),
            pltpu.VMEM((hops + 1, blocks, LANES), f32),
            pltpu.VMEM((hops, blocks, LANES), f32),
            dma((2, chunks)),
            dma((4,)),
            dma((m, SUB)),
            dma((m, SUB)),
            dma((m, SUB)),
            dma((m, SUB)),
            dma((m, SUB)),
            dma((hops,)),
            dma((hops,)),
        ],
        compiler_params=pltpu.CompilerParams(
            collective_id=0, has_side_effects=True, vmem_limit_bytes=VMEM_GRANT
        ),
        name="exchange",
    )(ranks, features, out_grads, cold_sums, weight, moment, second)
    new_weight, new_moment, new_second, new_cold = pl.pallas_call(
        functools.partial(update_kernel, n, rows * reps, tokens, hot),
        out_shape=(
            jax.ShapeDtypeStruct(weight.shape, f32),
            jax.ShapeDtypeStruct(weight.shape, f32),
            jax.ShapeDtypeStruct(weight.shape, f32),
            jax.ShapeDtypeStruct(cold_sums.shape, bf16),
        ),
        in_specs=[smem] + [vmem] * 6,
        out_specs=(hbm,) * 4,
        scratch_shapes=[pltpu.VMEM((3,) + weight.shape, f32), dma, dma((3,))],
        compiler_params=pltpu.CompilerParams(vmem_limit_bytes=VMEM_GRANT),
        name="update",
    )(ranks, summed, sq, kept, w, mo, se)
    return new_weight, new_moment, new_second, new_cold, sq.reshape(width)


def solution(mesh):
    owned = P(("rep", "dp"), None)
    placed = (P("dp", "rep"), P("dp", None), P("dp", "rep", None), owned, owned, owned, P())
    return jax.shard_map(
        functools.partial(body, mesh.shape["dp"], mesh.shape["rep"]),
        mesh=mesh,
        in_specs=placed,
        out_specs=(owned, owned, owned, P("dp", "rep", None), P()),
        check_vma=False,
    )
```

time: 147 us -> 106 us (0.72)
  Pallas kernels: 0 us -> 94.7 us
  blocking collectives: 43.8 us -> 0 us
  waiting for transfers between devices: 36.1 us -> 0 us
  matrix products: 16.2 us -> 0 us
  local copies, waits for them, and re-layouts: 26 us -> 10.2 us
  between operations: 14.1 us -> 0.66 us
  other arithmetic: 10.5 us -> 0 us
    pallas_call x0 -> x2, Pallas kernels: none -> 94.7 us  [the longest x1 91.1 us: body(): pl.pallas_call(functools.partial(exchange_kernel, n, reps, hot), out_shap...]
    psum x1 -> x0, blocking collectives: 43.8 us -> none  [body(): column_sq = lax.psum(partial_sq, ('dp', 'rep'))]
    reduce_scatter x1 -> x0, waiting for transfers between devices: 36.1 us -> none  [body(): lax.psum_scatter(packed.reshape(local_rows, hot_count * 128), 'dp', scatt...]
    dot_general x3 -> x0, matrix products: 16.2 us -> none  [the longest x1 8.02 us: body(): lax.dot_general(features, out_grads, (((0,), (0,)), ((), ())), preferred_...]
    reshape x2 -> x0, local copies, waits for them, and re-layouts: 10.5 us -> none  [the longest x1 9.3 us: body(): local.reshape(local_rows, blocks, 128)]
    broadcast_in_dim x1 -> x0, other arithmetic: 5.88 us -> none  [body(): jnp.where(hot_col[None, :], jnp.float32(0.0), local).astype(jnp.bfloat16)]
    unnamed x9 -> x15, local copies, waits for them, and re-layouts: 15.4 us -> 10.2 us
    select_n x1 -> x0, other arithmetic: 4.64 us -> none  [body(): new_second = jnp.where(hot_col[None, :], squared, second)]
  transfers between devices with their start and end apart: 1 -> 0, of which waited for: 1 -> 0; matrix products, arithmetic and copies ran while one was open for 8% -> 0% of each run, Pallas kernels for 0% -> 0%
where the time goes in v1:
time: 106 us
  Pallas kernels  94.7 us (89%)
  local copies, waits for them, and re-layouts  10.2 us (10%)
    pallas_call x1, Pallas kernels, body(): pl.pallas_call(functools.partial(exchange_kernel, n, reps, hot), out_shap...  91.1 us
    unnamed x15, local copies, waits for them, and re-layouts  10.2 us
    pallas_call x1, Pallas kernels, body(): pl.pallas_call(functools.partial(update_kernel, n, rows * reps, tokens, h...  3.56 us

profile of v1, /device:TPU:0, one launch (start us, length us, event | category | flops | bytes accessed | tf_op | source)
XLA Modules:
  0.0 105.5 jit_solution(8448028457647177529)
XLA Ops:
  0.6 0.0 copy-start
  0.6 2.2 %copy-done = bf16[1,2048,1024]{2,1,0:T(8,128)(2,1)S(1)} copy-done((bf16[1,2048,1024]{2,1,0:T(8,128)(2,1)S(1)}, bf16[1,2048,1024]{2,1,0:T(8,128)(2,1)}, u32[]{:S(2)}) %copy-start) | copy-done | bytes 4194328
  2.8 0.0 copy-start.1
  2.8 1.7 %copy-done.1 = bf16[640,2048]{1,0:T(8,128)(2,1)S(1)} copy-done((bf16[640,2048]{1,0:T(8,128)(2,1)S(1)}, bf16[640,2048]{1,0:T(8,128)(2,1)}, u32[]{:S(2)}) %copy-start.1) | copy-done | bytes 2621464
  4.6 0.0 copy-start.2
  4.6 1.3 %copy-done.2 = bf16[640,1024]{1,0:T(8,128)(2,1)S(1)} copy-done((bf16[640,1024]{1,0:T(8,128)(2,1)S(1)}, bf16[640,1024]{1,0:T(8,128)(2,1)}, u32[]{:S(2)}) %copy-start.2) | copy-done | bytes 1310744
  5.9 0.0 copy-start.3
  5.9 1.2 %copy-done.3 = f32[256,1024]{1,0:T(8,128)S(1)} copy-done((f32[256,1024]{1,0:T(8,128)S(1)}, f32[256,1024]{1,0:T(8,128)}, u32[]{:S(2)}) %copy-start.3) | copy-done | bytes 1048600
  7.1 0.0 copy-start.4
  7.1 1.2 %copy-done.4 = f32[256,1024]{1,0:T(8,128)S(1)} copy-done((f32[256,1024]{1,0:T(8,128)S(1)}, f32[256,1024]{1,0:T(8,128)}, u32[]{:S(2)}) %copy-start.4) | copy-done | bytes 1048600
  8.3 0.0 copy-start.5
  8.3 1.2 %copy-done.5 = f32[256,1024]{1,0:T(8,128)S(1)} copy-done((f32[256,1024]{1,0:T(8,128)S(1)}, f32[256,1024]{1,0:T(8,128)}, u32[]{:S(2)}) %copy-start.5) | copy-done | bytes 1048600
  9.6 0.0 copy-start.6
  9.6 0.7 copy-done.6
  10.2 91.1 %exchange.1 = (f32[256,512]{1,0:T(8,128)S(1)}, f32[8,128]{1,0:T(8,128)S(1)}, bf16[1,2048,1024]{2,1,0:T(8,128)(2,1)S(1)}, f32[256,1024]{1,0:T(8,128)S(1)}, f32[25...) custom-call(s32[8]{0:T(128)S(1)} %copy-done.6, bf16[640,2048]{1,0:T(8,128)(2,1)S(1)} %copy-done.1, ...), custom_call_target="tpu_custom_call" | custom-call | tf_op jit(solution)/shard_map/exchange/pallas_call | solution.py:331
  101.4 3.6 %update.1 = (f32[256,1024]{1,0:T(8,128)}, f32[256,1024]{1,0:T(8,128)}, f32[256,1024]{1,0:T(8,128)}, bf16[1,2048,1024]{2,1,0:T(8,128)(2,1)}) custom-call(s32[8]{0:T(128)S(1)} %copy-done.6, f32[256,512]{1,0:T(8,128)S(1)} %get-tuple-element.15.summed, f32[8,128]{1,0:T(8,128)S(1)} %get-tuple-element.16.sq, bf16[1,2048,1024]{2,1,0:T(8,128)(2,1)S(1)} %get-tuple-element.17.nc, ...), custom_call_target="tpu_custom_call" | custom-call | tf_op jit(solution)/shard_map/update/pallas_call | solution.py:369
  104.9 0.6 copy.13
Async XLA Ops:
  0.6 2.2 %copy-start = (bf16[1,2048,1024]{2,1,0:T(8,128)(2,1)S(1)}, bf16[1,2048,1024]{2,1,0:T(8,128)(2,1)}, u32[]{:S(2)}) copy-start(bf16[1,2048,1024]{2,1,0:T(8,128)(2,1)} %cold.1) | copy-start | bytes 12582916
  2.8 1.7 %copy-start.1 = (bf16[640,2048]{1,0:T(8,128)(2,1)S(1)}, bf16[640,2048]{1,0:T(8,128)(2,1)}, u32[]{:S(2)}) copy-start(bf16[640,2048]{1,0:T(8,128)(2,1)} %feat.1) | copy-start | bytes 7864324
  4.6 1.3 %copy-start.2 = (bf16[640,1024]{1,0:T(8,128)(2,1)S(1)}, bf16[640,1024]{1,0:T(8,128)(2,1)}, u32[]{:S(2)}) copy-start(bf16[640,1024]{1,0:T(8,128)(2,1)} %og.1) | copy-start | bytes 3932164
  5.9 1.2 %copy-start.3 = (f32[256,1024]{1,0:T(8,128)S(1)}, f32[256,1024]{1,0:T(8,128)}, u32[]{:S(2)}) copy-start(f32[256,1024]{1,0:T(8,128)} %weight.1) | copy-start | bytes 3145732
  7.1 1.2 %copy-start.4 = (f32[256,1024]{1,0:T(8,128)S(1)}, f32[256,1024]{1,0:T(8,128)}, u32[]{:S(2)}) copy-start(f32[256,1024]{1,0:T(8,128)} %moment.1) | copy-start | bytes 3145732
  8.3 1.2 %copy-start.5 = (f32[256,1024]{1,0:T(8,128)S(1)}, f32[256,1024]{1,0:T(8,128)}, u32[]{:S(2)}) copy-start(f32[256,1024]{1,0:T(8,128)} %second.1) | copy-start | bytes 3145732
  9.6 0.7 copy-start.6

commit v2 on v1

--- a/solution.py
+++ b/solution.py
@@ -9,6 +9,7 @@
 LANES = 128
 SUB = 2
 VMEM_GRANT = 30 * 2**20
+EXCHANGE_GRANT = 55 * 2**20
 MESH = pl.DeviceIdType.MESH
 
 
@@ -25,8 +26,8 @@
     n, reps, hot,
     ranks, feat, og, cold, weight, moment, second,
     summed, sq_out, nc_out, w_out, m_out, s_out,
-    feat_v, og_v, cold_v, local, pack, rx, lbuf, rbuf, hsrc, hbuf,
-    in_sem, state_sem, send1, recv1, zsend, lrecv, rrecv, hsend, hrecv,
+    feat_v, og_v, cold_v, local, pack, rx, lbuf, rbuf, hsrc, hbuf, gbuf,
+    in_sem, state_sem, send1, recv1, zsend, lrecv, rrecv, hsend, hrecv, gsend, grecv,
 ):
     m = n // 2
     rows, width = cold.shape[1], cold.shape[2]
@@ -40,8 +41,7 @@
     x = me % 2
     p = me // 2
     partner = me + 1 - 2 * x
-    dp_bits, rep_bits = bits_of(n), bits_of(reps)
-    steps = [("dp", b) for b in range(dp_bits)] + [("rep", b) for b in range(rep_bits)]
+    rep_bits = bits_of(reps)
 
     half = max(m // 2, 1)
     flip = p // half if m > 1 else 0
@@ -63,23 +63,20 @@
         side = i // m
         return 2 * dest(k) + (1 - side) * (1 - x) + side * x
 
-    def hop(axis, b):
-        index = me if axis == "dp" else rep
-        return {axis: flipped(index, b)}
-
     barrier = pltpu.get_barrier_semaphore()
-    pl.semaphore_signal(barrier, inc=1, device_id={"dp": partner}, device_id_type=MESH)
-
-    @pl.when(p > 0)
-    def _():
-        pl.semaphore_signal(barrier, inc=1, device_id={"dp": me - 2}, device_id_type=MESH)
-
-    @pl.when(p < m - 1)
-    def _():
-        pl.semaphore_signal(barrier, inc=1, device_id={"dp": me + 2}, device_id_type=MESH)
-
-    for axis, b in steps[1:]:
-        pl.semaphore_signal(barrier, inc=1, device_id=hop(axis, b), device_id_type=MESH)
+
+    def peer(o):
+        return (me + o) % n
+
+    def greet(o, carry):
+        pl.semaphore_signal(barrier, inc=1, device_id={"dp": peer(o)}, device_id_type=MESH)
+        return carry
+
+    lax.fori_loop(1, n, greet, 0)
+    for b in range(rep_bits):
+        pl.semaphore_signal(
+            barrier, inc=1, device_id={"rep": flipped(rep, b)}, device_id_type=MESH
+        )
 
     def feat_copy(i):
         c = chunk_at(i)
@@ -146,11 +143,24 @@
         return pltpu.make_async_remote_copy(
             src_ref=hsrc.at[s], dst_ref=hbuf.at[s],
             send_sem=hsend.at[s], recv_sem=hrecv.at[s],
-            device_id=hop(*steps[s]), device_id_type=MESH,
-        )
-
-    greeted = 1 + (len(steps) - 1) + (p + m - 1) // m + (2 * m - 2 - p) // m
-    pl.semaphore_wait(barrier, greeted)
+            device_id={"rep": flipped(rep, s)}, device_id_type=MESH,
+        )
+
+    def spread_copy(o):
+        return pltpu.make_async_remote_copy(
+            src_ref=gbuf.at[me], dst_ref=gbuf.at[me],
+            send_sem=gsend.at[o], recv_sem=grecv.at[me],
+            device_id={"dp": peer(o)}, device_id_type=MESH,
+        )
+
+    def arrival(j):
+        return pltpu.make_async_remote_copy(
+            src_ref=gbuf.at[j], dst_ref=gbuf.at[j],
+            send_sem=gsend.at[0], recv_sem=grecv.at[j],
+            device_id={"dp": partner}, device_id_type=MESH,
+        )
+
+    pl.semaphore_wait(barrier, n - 1 + rep_bits)
     state[3].wait()
 
     def compute(i, carry):
@@ -168,7 +178,7 @@
                 picked += local[:, b * LANES:(b + 1) * LANES] * picks[s][b]
             pack[at, s * LANES:(s + 1) * LANES] = picked
         if chunk == own:
-            @pl.when(i < m)
+            @pl.when(i < m - 1)
             def _():
                 for sub in range(SUB):
                     cross(i % m, sub).start()
@@ -186,8 +196,9 @@
                 cross(k, sub).start()
             return carry
 
-        lax.fori_loop(0, m, launch, 0)
-    norm_copy(0).start()
+        lax.fori_loop(0, m - 1, launch, 0)
+    if rep_bits:
+        norm_copy(0).start()
 
     def process(k, sub):
         d = dest(k)
@@ -219,29 +230,57 @@
             summed[sub * part:(sub + 1) * part] = pack[mine]
 
     def norm_step(s):
-        norm_copy(s).wait_recv()
-        hsrc[s + 1] = hsrc[s] + hbuf[s]
-        if s + 1 < len(steps):
-            norm_copy(s + 1).start()
+        if s < rep_bits:
+            norm_copy(s).wait_recv()
+            hsrc[s + 1] = hsrc[s] + hbuf[s]
+            if s + 1 < rep_bits:
+                norm_copy(s + 1).start()
+        if s == max(rep_bits, 1) - 1:
+            gbuf[me] = hsrc[rep_bits]
+
+            def spread(o, carry):
+                spread_copy(o).start()
+                return carry
+
+            lax.fori_loop(1, n, spread, 0)
+            for sub in range(SUB):
+                cross(m - 1, sub).start()
 
     done = 0
-    if m <= 8:
-        for k in range(m):
-            for sub in range(SUB):
-                if done < len(steps):
-                    norm_step(done)
-                    done += 1
-                process(k, sub)
-    else:
-        def walk(k, carry):
-            for sub in range(SUB):
-                process(k, sub)
-            return carry
-
-        lax.fori_loop(0, m, walk, 0)
-    for s in range(done, len(steps)):
+    norm_steps = max(rep_bits, 1)
+    if m == 1:
+        for s in range(norm_steps):
+            norm_step(s)
+        done = norm_steps
+    for k in range(min(m, 2)):
+        for sub in range(SUB):
+            process(k, sub)
+            if done < norm_steps:
+                norm_step(done)
+                done += 1
+    for s in range(done, norm_steps):
         norm_step(s)
-    sq_out[...] = hsrc[len(steps)]
+
+    def walk(k, carry):
+        for sub in range(SUB):
+            process(k, sub)
+        return carry
+
+    lax.fori_loop(min(m, 2), m, walk, 0)
+
+    def gather(o, carry):
+        arrival(peer(o)).wait_recv()
+        return carry
+
+    lax.fori_loop(1, n, gather, 0)
+
+    sq_out[...] = gbuf[0]
+
+    def total(j, carry):
+        sq_out[...] += gbuf[j]
+        return carry
+
+    lax.fori_loop(1, n, total, 0)
 
     for copy in state[:3]:
         copy.wait()
@@ -261,8 +300,14 @@
         return carry
 
     lax.fori_loop(0, m, drain, 0)
-    for s in range(len(steps)):
+    for s in range(rep_bits):
         norm_copy(s).wait_send()
+
+    def settle(o, carry):
+        spread_copy(o).wait_send()
+        return carry
+
+    lax.fori_loop(1, n, settle, 0)
 
 
 def update_kernel(
@@ -322,7 +367,7 @@
     own = rows // n
     chunk = max(own, LANES)
     chunks = rows // chunk
-    hops = bits_of(n) + bits_of(reps)
+    hops = max(bits_of(reps), 1)
     f32, bf16 = jnp.float32, jnp.bfloat16
     vmem = pl.BlockSpec(memory_space=pltpu.VMEM)
     smem = pl.BlockSpec(memory_space=pltpu.SMEM)
@@ -351,6 +396,7 @@
             pltpu.VMEM((m * own, packed), f32),
             pltpu.VMEM((hops + 1, blocks, LANES), f32),
             pltpu.VMEM((hops, blocks, LANES), f32),
+            pltpu.VMEM((n, blocks, LANES), f32),
             dma((2, chunks)),
             dma((4,)),
             dma((m, SUB)),
@@ -360,9 +406,11 @@
             dma((m, SUB)),
             dma((hops,)),
             dma((hops,)),
+            dma((n,)),
+            dma((n,)),
         ],
         compiler_params=pltpu.CompilerParams(
-            collective_id=0, has_side_effects=True, vmem_limit_bytes=VMEM_GRANT
+            collective_id=0, has_side_effects=True, vmem_limit_bytes=EXCHANGE_GRANT
         ),
         name="exchange",
     )(ranks, features, out_grads, cold_sums, weight, moment, second)

time: 106 us -> 60 us (0.57)
  Pallas kernels: 94.7 us -> 58.5 us
  local copies, waits for them, and re-layouts: 10.2 us -> 0.6 us
    pallas_call x1, Pallas kernels: 91.1 us -> 55 us  [body(): pl.pallas_call(functools.partial(exchange_kernel, n, reps, hot), out_shap...]
    unnamed x15 -> x3, local copies, waits for them, and re-layouts: 10.2 us -> 0.6 us
where the time goes in v2:
time: 60 us; the launch traced here: 59.8 us
  Pallas kernels  58.5 us (98%)
  between operations  0.67 us (1%)
  local copies, waits for them, and re-layouts  0.6 us (1%)
    pallas_call x1, Pallas kernels, body(): pl.pallas_call(functools.partial(exchange_kernel, n, reps, hot), out_shap...  55 us
    pallas_call x1, Pallas kernels, body(): pl.pallas_call(functools.partial(update_kernel, n, rows * reps, tokens, h...  3.56 us

profile of v2, /device:TPU:0, one launch (start us, length us, event | category | flops | bytes accessed | tf_op | source)
XLA Modules:
  0.0 59.8 jit_solution(16810065145705312219)
XLA Ops:
  0.6 0.0 copy-start
  0.6 55.0 %exchange.1 = (f32[256,512]{1,0:T(8,128)S(1)}, f32[8,128]{1,0:T(8,128)S(1)}, bf16[1,2048,1024]{2,1,0:T(8,128)(2,1)S(1)}, f32[256,1024]{1,0:T(8,128)S(1)}, f32[25...) custom-call(s32[8]{0:T(128)} %ranks.3, bf16[640,2048]{1,0:T(8,128)(2,1)} %feat.1, bf16[640,1024]{1,0:T(8,128)(2,1)} %og.1, ...), custom_call_target="tpu_custom_call" | custom-call | tf_op jit(solution)/shard_map/exchange/pallas_call | solution.py:376
  55.6 0.0 copy-done
  55.6 3.6 %update.1 = (f32[256,1024]{1,0:T(8,128)}, f32[256,1024]{1,0:T(8,128)}, f32[256,1024]{1,0:T(8,128)}, bf16[1,2048,1024]{2,1,0:T(8,128)(2,1)}) custom-call(s32[8]{0:T(128)S(1)} %copy-done, f32[256,512]{1,0:T(8,128)S(1)} %get-tuple-element.15.summed, f32[8,128]{1,0:T(8,128)S(1)} %get-tuple-element.16.sq, bf16[1,2048,1024]{2,1,0:T(8,128)(2,1)S(1)} %get-tuple-element.17.nc, ...), custom_call_target="tpu_custom_call" | custom-call | tf_op jit(solution)/shard_map/update/pallas_call | solution.py:417
  59.2 0.6 copy.13
Async XLA Ops:
  0.6 55.0 %copy-start = (s32[8]{0:T(128)S(1)}, s32[8]{0:T(128)}, u32[]{:S(2)}) copy-start(s32[8]{0:T(128)} %ranks.3) | copy-start | bytes 100

commit v3 on v2

--- a/solution.py
+++ b/solution.py
@@ -17,6 +17,13 @@
     return max(size.bit_length() - 1, 0)
 
 
+def split_rows(own):
+    late = max(own * 5 // 32 // 8, 1) * 8
+    early = own - late
+    cuts = [early * i // SUB // 8 * 8 for i in range(SUB)] + [early]
+    return early, late, cuts
+
+
 def flipped(index, bit):
     step = 1 << bit
     return index + step - 2 * step * ((index // step) % 2)
@@ -26,8 +33,9 @@
     n, reps, hot,
     ranks, feat, og, cold, weight, moment, second,
     summed, sq_out, nc_out, w_out, m_out, s_out,
-    feat_v, og_v, cold_v, local, pack, rx, lbuf, rbuf, hsrc, hbuf, gbuf,
+    feat_v, og_v, cold_v, local, pack, rx, lbuf, rbuf, packz, rxz, lbufz, rbufz, hsrc, hbuf, gbuf,
     in_sem, state_sem, send1, recv1, zsend, lrecv, rrecv, hsend, hrecv, gsend, grecv,
+    zzsend, zzleft, zzright, zxsend, zxrecv,
 ):
     m = n // 2
     rows, width = cold.shape[1], cold.shape[2]
@@ -35,7 +43,8 @@
     own = rows // n
     chunk = max(own, LANES)
     chunks = rows // chunk
-    part = own // SUB
+    early, late, cuts = split_rows(own)
+    group = chunk // own
     me = lax.axis_index("dp")
     rep = lax.axis_index("rep")
     x = me % 2
@@ -59,8 +68,8 @@
     def chunk_at(i):
         if chunk != own:
             return i
-        k = i % m
-        side = i // m
+        k = i // 2
+        side = i % 2
         return 2 * dest(k) + (1 - side) * (1 - x) + side * x
 
     barrier = pltpu.get_barrier_semaphore()
@@ -120,24 +129,59 @@
             row.append((1 - jnp.minimum(gap * gap, 1)).astype(jnp.float32))
         picks.append(row)
 
+    def rows_of(index, sub):
+        return pl.ds(pl.multiple_of(index * early + cuts[sub], 8), cuts[sub + 1] - cuts[sub])
+
     def cross(k, sub):
         d = dest(k)
-        src = pl.ds(pl.multiple_of((2 * d + 1 - x) * own + sub * part, 8), part)
-        dst = pl.ds(pl.multiple_of(d * own + sub * part, 8), part)
-        return pltpu.make_async_remote_copy(
-            src_ref=pack.at[src], dst_ref=rx.at[dst],
+        return pltpu.make_async_remote_copy(
+            src_ref=pack.at[rows_of(2 * d + 1 - x, sub)], dst_ref=rx.at[rows_of(d, sub)],
             send_sem=send1.at[d, sub], recv_sem=recv1.at[d, sub],
             device_id={"dp": partner}, device_id_type=MESH,
         )
 
     def along(d, sub, right):
-        src = pl.ds(pl.multiple_of((2 * d + x) * own + sub * part, 8), part)
-        dst = pl.ds(pl.multiple_of(d * own + sub * part, 8), part)
-        return pltpu.make_async_remote_copy(
-            src_ref=pack.at[src], dst_ref=(lbuf if right else rbuf).at[dst],
+        return pltpu.make_async_remote_copy(
+            src_ref=pack.at[rows_of(2 * d + x, sub)],
+            dst_ref=(lbuf if right else rbuf).at[rows_of(d, sub)],
             send_sem=zsend.at[d, sub], recv_sem=(lrecv if right else rrecv).at[d, sub],
             device_id={"dp": me + 2 if right else me - 2}, device_id_type=MESH,
         )
+
+    def whole_along(d, right):
+        return pltpu.make_async_remote_copy(
+            src_ref=packz.at[d], dst_ref=(lbufz if right else rbufz).at[d],
+            send_sem=zzsend.at[d], recv_sem=(zzleft if right else zzright).at[d],
+            device_id={"dp": me + 2 if right else me - 2}, device_id_type=MESH,
+        )
+
+    def whole_cross():
+        return pltpu.make_async_remote_copy(
+            src_ref=packz.at[p, pl.ds(pl.multiple_of((1 - x) * late, 8), late)],
+            dst_ref=rxz, send_sem=zxsend, recv_sem=zxrecv,
+            device_id={"dp": partner}, device_id_type=MESH,
+        )
+
+    def whole_step(k):
+        d = dest(k)
+
+        @pl.when(jnp.logical_and(d >= p, p > 0))
+        def _():
+            whole_along(d, True).wait_recv()
+            packz[d] += lbufz[d]
+
+        @pl.when(jnp.logical_and(d <= p, p < m - 1))
+        def _():
+            whole_along(d, False).wait_recv()
+            packz[d] += rbufz[d]
+
+        @pl.when(d > p)
+        def _():
+            whole_along(d, True).start()
+
+        @pl.when(d < p)
+        def _():
+            whole_along(d, False).start()
 
     def norm_copy(s):
         return pltpu.make_async_remote_copy(
@@ -176,17 +220,32 @@
             picked = local[:, :LANES] * picks[s][0]
             for b in range(1, blocks):
                 picked += local[:, b * LANES:(b + 1) * LANES] * picks[s][b]
-            pack[at, s * LANES:(s + 1) * LANES] = picked
+            lanes = slice(s * LANES, (s + 1) * LANES)
+            for g in range(group):
+                j = c * group + g
+                top = g * own
+                pack[pl.ds(pl.multiple_of(j * early, 8), early), lanes] = (
+                    picked[top:top + early]
+                )
+                packz[j // 2, pl.ds(pl.multiple_of(j % 2 * late, 8), late), lanes] = (
+                    picked[top + early:top + own]
+                )
         if chunk == own:
-            @pl.when(i < m - 1)
+            @pl.when(jnp.logical_and(i < chunks - 2, i % 2 == 0))
             def _():
                 for sub in range(SUB):
-                    cross(i % m, sub).start()
+                    cross(i // 2, sub).start()
+
         for b in range(blocks):
             cols = slice(b * LANES, (b + 1) * LANES)
             values = local[:, cols]
             hsrc[0, b:b + 1, :] += jnp.sum(values * values, axis=0, keepdims=True)
             nc_out[0, at, cols] = (values * keep[b]).astype(jnp.bfloat16)
+        if chunk == own:
+            @pl.when(jnp.logical_and(i < chunks - 2, i % 2 == 1))
+            def _():
+                whole_step(i // 2)
+
         return carry
 
     lax.fori_loop(0, chunks, compute, 0)
@@ -194,6 +253,7 @@
         def launch(k, carry):
             for sub in range(SUB):
                 cross(k, sub).start()
+            whole_step(k)
             return carry
 
         lax.fori_loop(0, m - 1, launch, 0)
@@ -202,8 +262,8 @@
 
     def process(k, sub):
         d = dest(k)
-        mine = pl.ds(pl.multiple_of((2 * d + x) * own + sub * part, 8), part)
-        slot = pl.ds(pl.multiple_of(d * own + sub * part, 8), part)
+        mine = rows_of(2 * d + x, sub)
+        slot = rows_of(d, sub)
         cross(k, sub).wait_recv()
         pack[mine] += rx[slot]
 
@@ -227,7 +287,7 @@
 
         @pl.when(d == p)
         def _():
-            summed[sub * part:(sub + 1) * part] = pack[mine]
+            summed[cuts[sub]:cuts[sub + 1]] = pack[mine]
 
     def norm_step(s):
         if s < rep_bits:
@@ -266,7 +326,11 @@
             process(k, sub)
         return carry
 
+    whole_step(m - 1)
+    whole_cross().start()
     lax.fori_loop(min(m, 2), m, walk, 0)
+    whole_cross().wait_recv()
+    summed[early:own] = packz[p, pl.ds(pl.multiple_of(x * late, 8), late)] + rxz[...]
 
     def gather(o, carry):
         arrival(peer(o)).wait_recv()
@@ -300,6 +364,21 @@
         return carry
 
     lax.fori_loop(0, m, drain, 0)
+    whole_cross().wait_send()
+
+    def drain_whole(k, carry):
+        d = dest(k)
+
+        @pl.when(d > p)
+        def _():
+            whole_along(d, True).wait_send()
+
+        @pl.when(d < p)
+        def _():
+            whole_along(d, False).wait_send()
+        return carry
+
+    lax.fori_loop(0, m, drain_whole, 0)
     for s in range(rep_bits):
         norm_copy(s).wait_send()
 
@@ -367,6 +446,7 @@
     own = rows // n
     chunk = max(own, LANES)
     chunks = rows // chunk
+    early, late, _ = split_rows(own)
     hops = max(bits_of(reps), 1)
     f32, bf16 = jnp.float32, jnp.bfloat16
     vmem = pl.BlockSpec(memory_space=pltpu.VMEM)
@@ -390,10 +470,14 @@
             pltpu.VMEM((tokens, width), bf16),
             pltpu.VMEM((chunks, chunk, width), bf16),
             pltpu.VMEM((chunk, width), f32),
-            pltpu.VMEM((rows, packed), f32),
-            pltpu.VMEM((m * own, packed), f32),
-            pltpu.VMEM((m * own, packed), f32),
-            pltpu.VMEM((m * own, packed), f32),
+            pltpu.VMEM((n * early, packed), f32),
+            pltpu.VMEM((m * early, packed), f32),
+            pltpu.VMEM((m * early, packed), f32),
+            pltpu.VMEM((m * early, packed), f32),
+            pltpu.VMEM((m, 2 * late, packed), f32),
+            pltpu.VMEM((late, packed), f32),
+            pltpu.VMEM((m, 2 * late, packed), f32),
+            pltpu.VMEM((m, 2 * late, packed), f32),
             pltpu.VMEM((hops + 1, blocks, LANES), f32),
             pltpu.VMEM((hops, blocks, LANES), f32),
             pltpu.VMEM((n, blocks, LANES), f32),
@@ -408,6 +492,11 @@
             dma((hops,)),
             dma((n,)),
             dma((n,)),
+            dma((m,)),
+            dma((m,)),
+            dma((m,)),
+            dma,
+            dma,
         ],
         compiler_params=pltpu.CompilerParams(
             collective_id=0, has_side_effects=True, vmem_limit_bytes=EXCHANGE_GRANT

time: 60 us -> 57.2 us (0.953)
  Pallas kernels: 58.5 us -> 55.8 us
    pallas_call x1, Pallas kernels: 55 us -> 52.2 us  [body(): pl.pallas_call(functools.partial(exchange_kernel, n, reps, hot), out_shap...]
where the time goes in v3:
time: 57.2 us; the launch traced here: 57 us
  Pallas kernels  55.8 us (98%)
  between operations  0.67 us (1%)
  local copies, waits for them, and re-layouts  0.6 us (1%)
    pallas_call x1, Pallas kernels, body(): pl.pallas_call(functools.partial(exchange_kernel, n, reps, hot), out_shap...  52.2 us
    pallas_call x1, Pallas kernels, body(): pl.pallas_call(functools.partial(update_kernel, n, rows * reps, tokens, h...  3.56 us

profile of v3, /device:TPU:0, one launch (start us, length us, event | category | flops | bytes accessed | tf_op | source)
XLA Modules:
  0.0 57.0 jit_solution(16483066075895800113)
XLA Ops:
  0.6 0.0 copy-start
  0.6 52.2 %exchange.1 = (f32[256,512]{1,0:T(8,128)S(1)}, f32[8,128]{1,0:T(8,128)S(1)}, bf16[1,2048,1024]{2,1,0:T(8,128)(2,1)S(1)}, f32[256,1024]{1,0:T(8,128)S(1)}, f32[25...) custom-call(s32[8]{0:T(128)} %ranks.3, bf16[640,2048]{1,0:T(8,128)(2,1)} %feat.1, bf16[640,1024]{1,0:T(8,128)(2,1)} %og.1, ...), custom_call_target="tpu_custom_call" | custom-call | tf_op jit(solution)/shard_map/exchange/pallas_call | solution.py:456
  52.9 0.0 copy-done
  52.9 3.6 %update.1 = (f32[256,1024]{1,0:T(8,128)}, f32[256,1024]{1,0:T(8,128)}, f32[256,1024]{1,0:T(8,128)}, bf16[1,2048,1024]{2,1,0:T(8,128)(2,1)}) custom-call(s32[8]{0:T(128)S(1)} %copy-done, f32[256,512]{1,0:T(8,128)S(1)} %get-tuple-element.15.summed, f32[8,128]{1,0:T(8,128)S(1)} %get-tuple-element.16.sq, bf16[1,2048,1024]{2,1,0:T(8,128)(2,1)S(1)} %get-tuple-element.17.nc, ...), custom_call_target="tpu_custom_call" | custom-call | tf_op jit(solution)/shard_map/update/pallas_call | solution.py:506
  56.4 0.6 %copy.13 = f32[1024]{0:T(1024)} copy(f32[1024]{0:T(1024)S(1)} %bitcast.1) | data formatting | bytes 8192
Async XLA Ops:
  0.6 52.2 %copy-start = (s32[8]{0:T(128)S(1)}, s32[8]{0:T(128)}, u32[]{:S(2)}) copy-start(s32[8]{0:T(128)} %ranks.3) | copy-start | bytes 100

commit v4 on v3

--- a/solution.py
+++ b/solution.py
@@ -18,7 +18,7 @@
 
 
 def split_rows(own):
-    late = max(own * 5 // 32 // 8, 1) * 8
+    late = max(own * 3 // 32 // 8, 1) * 8
     early = own - late
     cuts = [early * i // SUB // 8 * 8 for i in range(SUB)] + [early]
     return early, late, cuts
@@ -392,13 +392,15 @@
 def update_kernel(
     n, total_rows, tokens, hot,
     ranks, summed, sq, nc, weight, moment, second,
-    w_hbm, m_hbm, s_hbm, nc_hbm,
-    fresh, nc_sem, sem,
+    w_hbm, m_hbm, s_hbm, nc_hbm, sq_hbm,
+    fresh, nc_sem, sq_sem, sem,
 ):
     rows, width = weight.shape
     blocks = width // LANES
     cold_out = pltpu.make_async_copy(nc, nc_hbm, nc_sem)
     cold_out.start()
+    sq_out = pltpu.make_async_copy(sq, sq_hbm, sq_sem)
+    sq_out.start()
     for b in range(blocks):
         cols = slice(b * LANES, (b + 1) * LANES)
         slot = ranks[b]
@@ -433,6 +435,7 @@
         copy.start()
     for copy in copies:
         copy.wait()
+    sq_out.wait()
     cold_out.wait()
 
 
@@ -503,21 +506,22 @@
         ),
         name="exchange",
     )(ranks, features, out_grads, cold_sums, weight, moment, second)
-    new_weight, new_moment, new_second, new_cold = pl.pallas_call(
+    new_weight, new_moment, new_second, new_cold, norms = pl.pallas_call(
         functools.partial(update_kernel, n, rows * reps, tokens, hot),
         out_shape=(
             jax.ShapeDtypeStruct(weight.shape, f32),
             jax.ShapeDtypeStruct(weight.shape, f32),
             jax.ShapeDtypeStruct(weight.shape, f32),
             jax.ShapeDtypeStruct(cold_sums.shape, bf16),
+            jax.ShapeDtypeStruct((blocks, LANES), f32),
         ),
         in_specs=[smem] + [vmem] * 6,
-        out_specs=(hbm,) * 4,
-        scratch_shapes=[pltpu.VMEM((3,) + weight.shape, f32), dma, dma((3,))],
+        out_specs=(hbm,) * 5,
+        scratch_shapes=[pltpu.VMEM((3,) + weight.shape, f32), dma, dma, dma((3,))],
         compiler_params=pltpu.CompilerParams(vmem_limit_bytes=VMEM_GRANT),
         name="update",
     )(ranks, summed, sq, kept, w, mo, se)
-    return new_weight, new_moment, new_second, new_cold, sq.reshape(width)
+    return new_weight, new_moment, new_second, new_cold, norms.reshape(width)
 
 
 def solution(mesh):

time: 57.2 us -> 56.3 us (0.984)
  local copies, waits for them, and re-layouts: 0.6 us -> 0.01 us
    unnamed x3 -> x2, local copies, waits for them, and re-layouts: 0.6 us -> 0.01 us
where the time goes in v4:
time: 56.3 us; the launch traced here: 56.2 us
  Pallas kernels  55.5 us (99%)
  between operations  0.66 us (1%)
    pallas_call x1, Pallas kernels, body(): pl.pallas_call(functools.partial(exchange_kernel, n, reps, hot), out_shap...  51.9 us
    pallas_call x1, Pallas kernels, body(): pl.pallas_call(functools.partial(update_kernel, n, rows * reps, tokens, h...  3.57 us

profile of v4, /device:TPU:0, one launch (start us, length us, event | category | flops | bytes accessed | tf_op | source)
XLA Modules:
  0.0 56.2 jit_solution(18194347231707140680)
XLA Ops:
  0.6 0.0 copy-start
  0.6 51.9 %exchange.1 = (f32[256,512]{1,0:T(8,128)S(1)}, f32[8,128]{1,0:T(8,128)S(1)}, bf16[1,2048,1024]{2,1,0:T(8,128)(2,1)S(1)}, f32[256,1024]{1,0:T(8,128)S(1)}, f32[25...) custom-call(s32[8]{0:T(128)} %ranks.3, bf16[640,2048]{1,0:T(8,128)(2,1)} %feat.1, bf16[640,1024]{1,0:T(8,128)(2,1)} %og.1, ...), custom_call_target="tpu_custom_call" | custom-call | tf_op jit(solution)/shard_map/exchange/pallas_call | solution.py:459
  52.6 0.0 copy-done
  52.6 3.6 %update.1 = (f32[256,1024]{1,0:T(8,128)}, f32[256,1024]{1,0:T(8,128)}, f32[256,1024]{1,0:T(8,128)}, bf16[1,2048,1024]{2,1,0:T(8,128)(2,1)}, f32[8,128]{1,0:T(8,128)}) custom-call(s32[8]{0:T(128)S(1)} %copy-done, f32[256,512]{1,0:T(8,128)S(1)} %get-tuple-element.16.summed, f32[8,128]{1,0:T(8,128)S(1)} %get-tuple-element.17.sq, ...), custom_call_target="tpu_custom_call" | custom-call | tf_op jit(solution)/shard_map/update/pallas_call | solution.py:509
Async XLA Ops:
  0.6 51.9 %copy-start = (s32[8]{0:T(128)S(1)}, s32[8]{0:T(128)}, u32[]{:S(2)}) copy-start(s32[8]{0:T(128)} %ranks.3) | copy-start | bytes 100
